TPU v7x, 32 devices: a whole 2x2x4 slice. The times are simulated.
32 devices in a mesh: dp: 4 (over y, x), expert: 8 (over z, core).
Axes of the slice: x: 2, y: 2, z: 4, core: 2. Of those that a mesh axis runs over, the one named last changes fastest.
Arguments:
- tokens: bfloat16 [8, 512, 4096], P('expert', 'dp'), may hold values from -6 to 6
- w_gate: bfloat16 [8, 4096, 896], P('expert'), may hold values from -0.09375 to 0.09375
- w_up: bfloat16 [8, 4096, 896], P('expert'), may hold values from -0.09375 to 0.09375
- w_down: bfloat16 [8, 896, 4096], P('expert'), may hold values from -0.1875 to 0.1875
- expert_ids: int32 [8, 512, 4], P('expert'), may hold values from 0 to 7, all different within a row
- gate_index: int32 [8, 512, 4], P('expert'), may hold values from 0 to 255
- gate_table: float32 [256], replicated, may hold values from 0.05 to 1
- spill: int32 [8, 512], P('expert'), may hold values from 0 to 3, as said below
Outputs:
- mixed: bfloat16 [8, 512, 4096], P('expert', 'dp')
Inputs may be any that keep to these rules, and one draw needn't show every extreme that they name: `spill`: A token is dispatched by a device of its own column. Of the 128 tokens of one device at most 32 are dispatched by any one other device, and in every draw some device hands exactly 32 to some peer.
All inputs are finite; a program needn't handle non-finite values.
Results may differ from a plain program's by a relative error of at most 0.0058.
Values may be sent and summed in bfloat16 or wider, within the bound.
A program may use at most 128 MiB of HBM per device.

v0:
```python
import jax
import jax.numpy as jnp
from jax import lax
from jax.sharding import PartitionSpec as P


def local(tokens, w_gate, w_up, w_down, expert_ids, gate_index, gate_table, spill):
    dp_count = lax.axis_size("dp")
    expert_count = lax.axis_size("expert")
    local_experts = w_gate.shape[0]
    experts_all = local_experts * expert_count
    own_rows = tokens.shape[1]
    model_width = tokens.shape[2]
    column_tokens = spill.shape[1]
    top_count = expert_ids.shape[2]
    capacity = 3 * own_rows * top_count // (2 * experts_all)
    spill_room = own_rows // 4
    dp_index = lax.axis_index("dp")
    senders = spill[0]
    flat_ids = expert_ids[0].reshape(-1)
    level_count = gate_table.shape[0]
    matches = gate_index[0][:, :, None] == jnp.arange(level_count, dtype=jnp.int32)
    picked = jnp.sum(jnp.where(matches, gate_table, 0.0), axis=2)
    weight = picked / jnp.sum(picked, axis=1, keepdims=True)
    pair_sender = jnp.repeat(senders, top_count)
    is_mine = pair_sender == dp_index
    onehot = (
        (flat_ids[:, None] == jnp.arange(experts_all, dtype=jnp.int32)) & is_mine[:, None]
    ).astype(jnp.int32)
    slot_rank = jnp.sum((jnp.cumsum(onehot, axis=0) - onehot) * onehot, axis=1)
    is_kept = is_mine & (slot_rank < capacity)
    empty_slot = experts_all * capacity
    slot_index = jnp.where(is_kept, flat_ids * capacity + slot_rank, empty_slot)
    pair_token = jnp.arange(column_tokens * top_count, dtype=jnp.int32) // top_count
    zero_row = jnp.zeros((1, model_width), tokens.dtype)
    token_ids = jnp.arange(column_tokens, dtype=jnp.int32)
    home_dev = token_ids // own_rows
    local_token = token_ids - home_dev * own_rows
    is_moved = senders != home_dev
    route_key = home_dev * dp_count + senders
    route_hot = (route_key[:, None] == jnp.arange(dp_count * dp_count, dtype=jnp.int32)).astype(
        jnp.int32
    )
    spill_rank = jnp.sum((jnp.cumsum(route_hot, axis=0) - route_hot) * route_hot, axis=1)
    incoming = is_moved & (senders == dp_index)
    spill_slots = dp_count * spill_room
    outgoing = is_moved & (home_dev == dp_index)
    send_target = jnp.where(outgoing, senders * spill_room + spill_rank, spill_slots)
    send_source = (
        jnp.full((spill_slots,), own_rows, jnp.int32).at[send_target].set(local_token, mode="drop")
    )
    own_padded = jnp.concatenate([tokens[0], zero_row], axis=0)
    outgoing_rows = own_padded[send_source].reshape(dp_count, spill_room, model_width)
    arrived = lax.all_to_all(outgoing_rows, "dp", split_axis=0, concat_axis=0, tiled=True)
    source_rows = jnp.concatenate(
        [tokens[0], arrived.reshape(spill_slots, model_width), zero_row], axis=0
    )
    token_row = jnp.where(
        home_dev == dp_index,
        local_token,
        jnp.where(incoming, own_rows + home_dev * spill_room + spill_rank, own_rows + spill_slots),
    )
    dispatch_source = (
        jnp.full((empty_slot,), source_rows.shape[0] - 1, jnp.int32)
        .at[slot_index]
        .set(token_row[pair_token], mode="drop")
    )
    outbound = source_rows[dispatch_source].reshape(
        expert_count, local_experts, capacity, model_width
    )
    block = lax.all_to_all(outbound, "expert", split_axis=0, concat_axis=0, tiled=True)
    gate_part = jnp.einsum("aecd,edf->aecf", block, w_gate, preferred_element_type=jnp.float32)
    up_part = jnp.einsum("aecd,edf->aecf", block, w_up, preferred_element_type=jnp.float32)
    hidden = (jax.nn.silu(gate_part) * up_part).astype(jnp.bfloat16)
    expert_out = jnp.einsum(
        "aecf,efd->aecd", hidden, w_down, preferred_element_type=jnp.float32
    ).astype(jnp.bfloat16)
    returned = lax.all_to_all(expert_out, "expert", split_axis=0, concat_axis=0, tiled=True)
    results = jnp.concatenate([returned.reshape(empty_slot, model_width), zero_row], axis=0)
    slot_grid = jnp.concatenate(
        [
            slot_index.reshape(column_tokens, top_count),
            jnp.full((1, top_count), empty_slot, jnp.int32),
        ],
        axis=0,
    )
    kept_scale = jnp.where(is_kept.reshape(column_tokens, top_count), weight, 0.0)
    scale_grid = jnp.concatenate([kept_scale, jnp.zeros((1, top_count), jnp.float32)], axis=0)

    def combine(chosen):
        chosen_slots = slot_grid[chosen]
        chosen_scale = scale_grid[chosen]
        summed = jnp.zeros((chosen.shape[0], model_width), jnp.float32)
        for member in range(top_count):
            summed = summed + chosen_scale[:, member : member + 1] * results[
                chosen_slots[:, member]
            ].astype(jnp.float32)
        return summed

    own_ids = dp_index * own_rows + jnp.arange(own_rows, dtype=jnp.int32)
    own_part = combine(own_ids)
    arrived_target = jnp.where(incoming, home_dev * spill_room + spill_rank, spill_slots)
    arrived_ids = (
        jnp.full((spill_slots,), column_tokens, jnp.int32)
        .at[arrived_target]
        .set(token_ids, mode="drop")
    )
    arrived_part = combine(arrived_ids).reshape(dp_count, spill_room, model_width)
    returned_part = lax.all_to_all(
        arrived_part.astype(jnp.bfloat16), "dp", split_axis=0, concat_axis=0, tiled=True
    ).astype(arrived_part.dtype)
    back_rows = jnp.concatenate(
        [returned_part.reshape(spill_slots, model_width), jnp.zeros((1, model_width), jnp.float32)],
        axis=0,
    )
    back_pick = jnp.where(
        is_moved[own_ids], senders[own_ids] * spill_room + spill_rank[own_ids], spill_slots
    )
    mixed = own_part + back_rows[back_pick]
    return mixed.astype(jnp.bfloat16)[None]


def solution(mesh):
    in_specs = (
        P("expert", "dp", None),
        P("expert", None, None),
        P("expert", None, None),
        P("expert", None, None),
        P("expert", None, None),
        P("expert", None, None),
        P(),
        P("expert", None),
    )
    out_specs = P("expert", "dp", None)
    return jax.shard_map(local, mesh=mesh, in_specs=in_specs, out_specs=out_specs, check_vma=False)
```

profile of v0, /device:TPU:0, one launch (start us, length us, event | category | flops | bytes accessed | tf_op | source)
XLA Modules:
  0.0 439.0 jit_solution(12729083998823400086)
XLA Ops:
  3.6 2.4 scatter_custom_fusion
  6.1 1.3 concatenate.21
  7.4 2.2 gather_fusion.1
  9.6 5.2 %all-to-all-start = ((bf16[4,32,4096]{2,1,0:T(8,128)(2,1)}), bf16[4,32,4096]{2,1,0:T(8,128)(2,1)S(1)}, u32[]{:S(2)}, u32[]{:S(2)}) async-start(bf16[4,32,4096]{2,1,0:T(8,128)(2,1)} %bitcast.10), calls=%async_computation | async-start | bytes 2097152 | tf_op jit(solution)/shard_map/all_to_all | solution.py:54
  16.0 2.3 reduce-window.14
  19.5 13.2 %gather_fusion.2 = s32[2048]{0:T(1024)S(1)} fusion(s32[512]{0:T(512)S(1)} %get-tuple-element.23, s32[2048]{0:T(1024)S(1)} %broadcast_clamp_fusion), kind=kCustom, calls=%fused_computation.2 | custom fusion | bytes 24576 | tf_op jit(solution)/shard_map/gather | solution.py:66
  32.7 8.0 %scatter_custom_fusion.1 = s32[768]{0:T(1024)S(1)} fusion(s32[2048]{0:T(1024)S(1)} %bitcast.192, s32[2048]{0:T(1024)S(1)} %gather_fusion.2, s32[]{:T(128)} %constant.90.clone.1), kind=kCustom, calls=%fused_computation.175 | custom fusion | bytes 3076 | tf_op jit(solution)/shard_map/scatter | solution.py:66
  41.8 1.8 maximum_maximum_fusion
  43.6 5.7 %gather_fusion.3 = bf16[768,4096]{1,0:T(8,128)(2,1)} fusion(bf16[257,4096]{1,0:T(8,128)(2,1)S(1)} %maximum_maximum_fusion, s32[1024]{0:T(1024)S(1)} %pad_clamp_fusion.11), kind=kCustom, calls=%fused_computation.3 | custom fusion | bytes 12585984 | tf_op jit(solution)/shard_map/gather | solution.py:68
  49.3 144.7 %all_to_all.20 = bf16[8,1,96,4096]{3,2,1,0:T(8,128)(2,1)S(1)} all-to-all(bf16[8,1,96,4096]{3,2,1,0:T(8,128)(2,1)} %bitcast.178), channel_id=1, replica_groups=mesh['dp'=4,'expert'=8] {'expert'}, dimensions={0} | all-to-all | bytes 12582912 | tf_op jit(solution)/shard_map/all_to_all | solution.py:71
  194.0 12.1 %fusion.2 = f32[8,96,896]{2,1,0:T(8,128)S(1)} fusion(bf16[1,4096,896]{2,1,0:T(8,128)(2,1)} %param.10, bf16[8,1,96,4096]{3,2,1,0:T(8,128)(2,1)S(1)} %all_to_all.20), kind=kOutput, calls=%fused_computation.24 | convolution fusion | flops 5637144576 | bytes 16384000 | tf_op jit(solution)/shard_map/aecd,edf->aecf/dot_general | solution.py:73
  206.2 6.9 %fusion.31 = bf16[8,96,896]{2,1,0:T(8,128)(2,1)S(1)} fusion(f32[8,96,896]{2,1,0:T(8,128)S(1)} %fusion.2, bf16[1,4096,896]{2,1,0:T(8,128)(2,1)S(1)} %bitcast.196, bf16[8,1,96,4096]{3,2,1,0:T(8,128)(2,1)S(1)} %all_to_all.20), kind=kOutput, calls=%fused_computation.60 | convolution fusion | flops 5641273344 | bytes 17760256 | tf_op jit(solution)/shard_map/aecd,edf->aecf/dot_general | solution.py:72
  213.1 8.5 %fusion.11 = bf16[8,1,96,4096]{3,2,1,0:T(8,128)(2,1)} fusion(bf16[8,96,896]{2,1,0:T(8,128)(2,1)S(1)} %fusion.31, bf16[1,896,4096]{2,1,0:T(8,128)(2,1)S(1)} %bitcast.198), kind=kOutput, calls=%fused_computation.31 | convolution fusion | flops 5640290304 | bytes 15007744 | tf_op jit(solution)/shard_map/aecf,efd->aecd/dot_general | solution.py:75
  221.6 4.7 %all-to-all-start.2 = ((bf16[8,1,96,4096]{3,2,1,0:T(8,128)(2,1)}), bf16[8,1,96,4096]{3,2,1,0:T(8,128)(2,1)}, u32[]{:S(2)}, u32[]{:S(2)}) async-start(bf16[8,1,96,4096]{3,2,1,0:T(8,128)(2,1)} %fusion.11), calls=%async_computation.2 | async-start | bytes 12582912 | tf_op jit(solution)/shard_map/all_to_all | solution.py:78
  226.5 1.3 gather_fusion.16
  227.8 1.3 gather_fusion.17
  229.7 2.4 scatter_custom_fusion.2
  235.9 1.4 gather_fusion.15
  238.3 126.9 %all-to-all-done.2 = bf16[8,1,96,4096]{3,2,1,0:T(8,128)(2,1)} async-done(((bf16[8,1,96,4096]{3,2,1,0:T(8,128)(2,1)}), bf16[8,1,96,4096]{3,2,1,0:T(8,128)(2,1)}, u32[]{:S(2)}, u32[]{:S(2)}) %all-to-all-start.2) | async-done | bytes 6291488 | tf_op jit(solution)/shard_map/all_to_all | solution.py:78
  365.3 6.2 %concatenate.23 = bf16[769,4096]{1,0:T(8,128)(2,1)} pad(bf16[768,4096]{1,0:T(8,128)(2,1)} %bitcast.37, bf16[]{:T(256)} %constant.82.clone.1), padding=0_1x0_0 | pad | bytes 12591106 | tf_op jit(solution)/shard_map/concatenate | solution.py:79
  371.5 5.8 %gather_fusion.14 = bf16[128,4096]{1,0:T(8,128)(2,1)S(1)} fusion(bf16[769,4096]{1,0:T(8,128)(2,1)} %concatenate.23, s32[1024]{0:T(1024)S(1)} %get-tuple-element.28), kind=kCustom, calls=%fused_computation.14 | custom fusion | bytes 2097664 | tf_op jit(solution)/shard_map/gather | solution.py:95
  377.4 5.8 %gather_fusion.13 = bf16[128,4096]{1,0:T(8,128)(2,1)S(1)} fusion(bf16[769,4096]{1,0:T(8,128)(2,1)} %concatenate.23, s32[1024]{0:T(1024)S(1)} %get-tuple-element.29), kind=kCustom, calls=%fused_computation.13 | custom fusion | bytes 2097664 | tf_op jit(solution)/shard_map/gather | solution.py:95
  383.2 5.8 %gather_fusion.12 = bf16[128,4096]{1,0:T(8,128)(2,1)S(1)} fusion(bf16[769,4096]{1,0:T(8,128)(2,1)} %concatenate.23, s32[1024]{0:T(1024)S(1)} %get-tuple-element.30), kind=kCustom, calls=%fused_computation.12 | custom fusion | bytes 2097664 | tf_op jit(solution)/shard_map/gather | solution.py:95
  389.0 6.8 %gather_fusion.11 = bf16[128,4096]{1,0:T(8,128)(2,1)} fusion(bf16[769,4096]{1,0:T(8,128)(2,1)} %concatenate.23, s32[1024]{0:T(1024)S(1)} %get-tuple-element.31), kind=kCustom, calls=%fused_computation.11 | custom fusion | bytes 2097664 | tf_op jit(solution)/shard_map/gather | solution.py:95
  395.8 3.6 fusion.19
  399.4 4.2 all-to-all-start.3
  404.1 6.8 %gather_fusion.8 = bf16[128,4096]{1,0:T(8,128)(2,1)} fusion(bf16[769,4096]{1,0:T(8,128)(2,1)} %concatenate.23, s32[1024]{0:T(1024)S(1)} %pad_clamp_fusion.7), kind=kCustom, calls=%fused_computation.8 | custom fusion | bytes 2097664 | tf_op jit(solution)/shard_map/gather | solution.py:95
  410.9 6.8 %gather_fusion.7 = bf16[128,4096]{1,0:T(8,128)(2,1)} fusion(bf16[769,4096]{1,0:T(8,128)(2,1)} %concatenate.23, s32[1024]{0:T(1024)S(1)} %pad_clamp_fusion.8), kind=kCustom, calls=%fused_computation.7 | custom fusion | bytes 2097664 | tf_op jit(solution)/shard_map/gather | solution.py:95
  417.8 6.9 %gather_fusion.6 = bf16[128,4096]{1,0:T(8,128)(2,1)} fusion(bf16[769,4096]{1,0:T(8,128)(2,1)} %concatenate.23, s32[1024]{0:T(1024)S(1)} %pad_clamp_fusion.9), kind=kCustom, calls=%fused_computation.6 | custom fusion | bytes 2097664 | tf_op jit(solution)/shard_map/gather | solution.py:95
  424.6 6.8 %gather_fusion.5 = bf16[128,4096]{1,0:T(8,128)(2,1)} fusion(bf16[769,4096]{1,0:T(8,128)(2,1)} %concatenate.23, s32[1024]{0:T(1024)S(1)} %pad_clamp_fusion.10), kind=kCustom, calls=%fused_computation.5 | custom fusion | bytes 2097664 | tf_op jit(solution)/shard_map/gather | solution.py:95
  431.6 2.6 gather_fusion.18
  434.2 4.5 %fusion.24 = bf16[1,128,4096]{2,1,0:T(8,128)(2,1)} fusion(f32[128,4096]{1,0:T(8,128)} %gather_fusion.18, bf16[128,4096]{1,0:T(8,128)(2,1)S(1)} %copy-done.3, bf16[128,4096]{1,0:T(8,128)(2,1)} %gather_fusion.7, bf16[128,4096]{1,0:T(8,128)(2,1)} %gather_fusion.6, bf16[128,4096]{1,0:T(8,128)(2,1)} %gather_fusion.5, f32[128]{0:T(128)S(1)} %get-tuple-element.8, ...), kind=kLoop, calls=%fused_computation.53 | loop fusion | flops 6815744 | bytes 7342080 | tf_op jit(solution)/shard_map/convert_element_type | solution.py:120
  (102 shorter events, 13.1 us)
Async XLA Ops:
  7.4 7.4 %copy-start = (s32[1,512]{1,0:T(1,128)S(1)}, s32[1,512]{1,0:T(1,128)}, u32[]{:S(2)}) copy-start(s32[1,512]{1,0:T(1,128)} %param.15) | copy-start | bytes 6148
  7.4 7.4 %copy-start.4 = (s32[1,512,4]{1,2,0:T(4,128)S(1)}, s32[1,512,4]{1,2,0:T(4,128)}, u32[]{:S(2)}) copy-start(s32[1,512,4]{1,2,0:T(4,128)} %param.12) | copy-start | bytes 24580
  9.6 31.2 %all-to-all-start = ((bf16[4,32,4096]{2,1,0:T(8,128)(2,1)}), bf16[4,32,4096]{2,1,0:T(8,128)(2,1)S(1)}, u32[]{:S(2)}, u32[]{:S(2)}) async-start(bf16[4,32,4096]{2,1,0:T(8,128)(2,1)} %bitcast.10), calls=%async_computation | async-start | bytes 2097152 | tf_op jit(solution)/shard_map/all_to_all | solution.py:54
  19.5 22.3 %copy-start.1 = (bf16[1,128,4096]{2,1,0:T(8,128)(2,1)S(1)}, bf16[1,128,4096]{2,1,0:T(8,128)(2,1)}, u32[]{:S(2)}) copy-start(bf16[1,128,4096]{2,1,0:T(8,128)(2,1)} %param.8) | copy-start | bytes 3145732
  40.8 1.0 copy-start.2
  49.3 156.8 %slice-start = ((s8[7340032]{0:T(1024)(128)(4,1)}), s8[4194304]{0:T(1024)(128)(4,1)S(1)}, s32[]{:S(2)}) async-start(s8[7340032]{0:T(1024)(128)(4,1)} %bitcast.195), calls=%async_computation.4 | async-start | bytes 8388608
  194.0 12.1 %slice-start.1 = ((s8[7340032]{0:T(1024)(128)(4,1)}), s8[3145728]{0:T(1024)(128)(4,1)S(1)}, s32[]{:S(2)}) async-start(s8[7340032]{0:T(1024)(128)(4,1)} %bitcast.195), calls=%async_computation.5 | async-start | bytes 6291456
  194.0 19.0 %slice-start.2 = ((s8[7340032]{0:T(1024)(128)(4,1)}), s8[4194304]{0:T(1024)(128)(4,1)S(1)}, s32[]{:S(2)}) async-start(s8[7340032]{0:T(1024)(128)(4,1)} %bitcast.197), calls=%async_computation.6 | async-start | bytes 8388608
  206.1 7.0 %slice-start.3 = ((s8[7340032]{0:T(1024)(128)(4,1)}), s8[3145728]{0:T(1024)(128)(4,1)S(1)}, s32[]{:S(2)}) async-start(s8[7340032]{0:T(1024)(128)(4,1)} %bitcast.197), calls=%async_computation.7 | async-start | bytes 6291456
  221.6 143.7 %all-to-all-start.2 = ((bf16[8,1,96,4096]{3,2,1,0:T(8,128)(2,1)}), bf16[8,1,96,4096]{3,2,1,0:T(8,128)(2,1)}, u32[]{:S(2)}, u32[]{:S(2)}) async-start(bf16[8,1,96,4096]{3,2,1,0:T(8,128)(2,1)} %fusion.11), calls=%async_computation.2 | async-start | bytes 12582912 | tf_op jit(solution)/shard_map/all_to_all | solution.py:78
  226.4 7.1 %copy-start.5 = (s32[1,512,4]{1,2,0:T(4,128)S(1)}, s32[1,512,4]{1,2,0:T(4,128)}, u32[]{:S(2)}) copy-start(s32[1,512,4]{1,2,0:T(4,128)} %param.13) | copy-start | bytes 24580
  226.4 7.1 %copy-start.6 = (f32[256]{0:T(256)S(1)}, f32[256]{0:T(256)}, u32[]{:S(2)}) copy-start(f32[256]{0:T(256)} %param.14) | copy-start | bytes 3076
  399.4 32.0 %all-to-all-start.3 = ((bf16[4,32,4096]{2,1,0:T(8,128)(2,1)}), bf16[4,32,4096]{2,1,0:T(8,128)(2,1)S(1)}, u32[]{:S(2)}, u32[]{:S(2)}) async-start(bf16[4,32,4096]{2,1,0:T(8,128)(2,1)} %fusion.19), calls=%async_computation.3 | async-start | bytes 2097152 | tf_op jit(solution)/shard_map/all_to_all | solution.py:109
  431.6 2.6 copy-start.3
where the time goes:
time: 445 us; the launch traced here: 439 us
  blocking collectives  145 us (33%)
  waiting for transfers between devices  127 us (29%)
  local copies, waits for them, and re-layouts  107 us (24%)
  matrix products  27.5 us (6%)
  other arithmetic  17.9 us (4%)
  starting transfers between devices  14.1 us (3%)
    all_to_all x1, blocking collectives, local(): lax.all_to_all(outbound, 'expert', split_axis=0, concat_axis=0, tiled=True)  145 us
    all_to_all x1, waiting for transfers between devices, local(): lax.all_to_all(expert_out, 'expert', split_axis=0, concat_axis=0, tiled=T...  127 us
    gather x8, local copies, waits for them, and re-layouts, combine(): results[chosen_slots[:, member]].astype(jnp.float32)  51.6 us
    gather x1, local copies, waits for them, and re-layouts, local(): token_row[pair_token]  13.2 us
    dot_general x1, matrix products, local(): jnp.einsum('aecd,edf->aecf', block, w_up, preferred_element_type=jnp.floa...  12.1 us
  transfers between devices with their start and end apart: 3, of which 1 were waited for; matrix products, arithmetic and copies ran while one was open for 15% of the time, Pallas kernels for 0%

commit v1 on v0

--- a/solution.py
+++ b/solution.py
@@ -1,10 +1,13 @@
+import functools
 import jax
 import jax.numpy as jnp
 from jax import lax
+from jax.experimental import pallas as pl
+from jax.experimental.pallas import tpu as pltpu
 from jax.sharding import PartitionSpec as P
 
 
-def local(tokens, w_gate, w_up, w_down, expert_ids, gate_index, gate_table, spill):
+def exchange_plan(tokens, w_gate, w_up, w_down, expert_ids, gate_index, gate_table, spill):
     dp_count = lax.axis_size("dp")
     expert_count = lax.axis_size("expert")
     local_experts = w_gate.shape[0]
@@ -120,6 +123,343 @@
     return mixed.astype(jnp.bfloat16)[None]
 
 
+CORES = 2
+CHUNKS = 8
+LAG = 2
+MESH = pl.DeviceIdType.MESH
+
+
+def token_scales(expert_ids, gate_index, gate_table, spill, own_rows, experts_all):
+    top_count = expert_ids.shape[2]
+    column_tokens = spill.shape[1]
+    capacity = 3 * own_rows * top_count // (2 * experts_all)
+    first = lax.axis_index("dp") * own_rows
+    senders = spill[0]
+    experts = jnp.arange(experts_all, dtype=jnp.int32)
+    hot = expert_ids[0][:, :, None] == experts
+    chosen = jnp.any(hot, axis=1)
+    own_senders = lax.dynamic_slice_in_dim(senders, first, own_rows)
+    own_tokens = first + jnp.arange(own_rows, dtype=jnp.int32)
+    earlier = (jnp.arange(column_tokens, dtype=jnp.int32)[None, :] < own_tokens[:, None]) & (
+        senders[None, :] == own_senders[:, None]
+    )
+    rank = jnp.dot(
+        earlier.astype(jnp.bfloat16), chosen.astype(jnp.bfloat16), preferred_element_type=jnp.float32
+    )
+    own_index = lax.dynamic_slice_in_dim(gate_index[0], first, own_rows)
+    levels = jnp.arange(gate_table.shape[0], dtype=jnp.int32)
+    picked = jnp.sum(jnp.where(own_index[:, :, None] == levels, gate_table, 0.0), axis=2)
+    weight = picked / jnp.sum(picked, axis=1, keepdims=True)
+    own_hot = lax.dynamic_slice_in_dim(hot, first, own_rows)
+    scale = jnp.sum(jnp.where(own_hot, weight[:, :, None], 0.0), axis=1)
+    return jnp.where(rank < capacity, scale, 0.0).T
+
+
+def line_kernel(
+    chips, tok, w_gate, w_up, w_down, scale, out,
+    x, w_in, w_out, scales, both, hid, part, near, from_left, from_right, going, total,
+    own_sem, sc_s, sc_r, ag_right, ag_left, ag_r, ag_sib, sib_r, part_s, part_r, go_s, left_r, right_r,
+):
+    own_rows, width = tok.shape[1], tok.shape[2]
+    hidden_units = w_gate.shape[2]
+    piece = own_rows // CHUNKS
+    count = chips * CORES
+    me = lax.axis_index("expert")
+    p = me // CORES
+    q = lax.rem(me, CORES)
+    sib = p * CORES + 1 - q
+    right, left = me + CORES, me - CORES
+    has_right, has_left = p < chips - 1, p > 0
+
+    def send(src, dst, send_sem, recv_sem, device):
+        return pltpu.make_async_remote_copy(
+            src_ref=src, dst_ref=dst, send_sem=send_sem, recv_sem=recv_sem,
+            device_id={"expert": device}, device_id_type=MESH,
+        )
+
+    def rows(c):
+        return pl.ds(pl.multiple_of(c * piece, piece), piece)
+
+    def gather_copy(s, c, sems, recv, device):
+        block = x.at[CORES * s + q, rows(c)]
+        return send(block, block, sems.at[s, c], recv.at[s, c], device)
+
+    loads = [
+        pltpu.make_async_copy(tok.at[0], x.at[me], own_sem.at[0]),
+        pltpu.make_async_copy(scale, scales.at[me], own_sem.at[1]),
+        pltpu.make_async_copy(w_gate.at[0], w_in.at[:, pl.ds(0, hidden_units)], own_sem.at[2]),
+        pltpu.make_async_copy(w_up.at[0], w_in.at[:, pl.ds(hidden_units, hidden_units)], own_sem.at[3]),
+        pltpu.make_async_copy(w_down.at[0], w_out, own_sem.at[4]),
+    ]
+    loads[0].start()
+    loads[1].start()
+    barrier = pltpu.get_barrier_semaphore()
+    for step in range(1, count):
+        pl.semaphore_signal(
+            barrier, inc=1, device_id={"expert": lax.rem(me + step, count)}, device_id_type=MESH
+        )
+    pl.semaphore_wait(barrier, count - 1)
+    loads[0].wait()
+
+    def first_sends(c, carry):
+        @pl.when(has_right)
+        def _():
+            gather_copy(p, c, ag_right, ag_r, right).start()
+
+        @pl.when(has_left)
+        def _():
+            gather_copy(p, c, ag_left, ag_r, left).start()
+
+        gather_copy(p, c, ag_sib, sib_r, sib).start()
+        return carry
+
+    lax.fori_loop(0, CHUNKS, first_sends, 0)
+    loads[1].wait()
+    for step in range(1, count):
+        send(
+            scale, scales.at[me], sc_s.at[step], sc_r.at[step], lax.rem(me + step, count)
+        ).start()
+    for load in loads[2:]:
+        load.start()
+    for load in loads[2:]:
+        load.wait()
+    for step in range(1, count):
+        send(
+            scale, scales.at[lax.rem(me - step + count, count)], sc_s.at[step], sc_r.at[step], sib
+        ).wait_recv()
+
+    tall = CORES * own_rows
+    in_tile = 2 * hidden_units // 7 if (2 * hidden_units) % 7 == 0 else 2 * hidden_units
+    out_tile = width // 8
+
+    def sib_wait(s):
+        def one(c, carry):
+            block = x.at[CORES * s + 1 - q, rows(c)]
+            send(block, block, ag_sib.at[s, c], sib_r.at[s, c], sib).wait_recv()
+            return carry
+
+        lax.fori_loop(0, CHUNKS, one, 0)
+
+    def expert(s):
+        def enter(t, carry):
+            cols = pl.ds(pl.multiple_of(t * in_tile, 128), in_tile)
+            tokens = x[pl.ds(CORES * s, CORES)].reshape(tall, width)
+            both[:, cols] = jnp.dot(tokens, w_in[:, cols], preferred_element_type=jnp.float32)
+            return carry
+
+        lax.fori_loop(0, 2 * hidden_units // in_tile, enter, 0)
+        for core in range(CORES):
+            part_rows = pl.ds(core * own_rows, own_rows)
+            row = scales[CORES * s + core, pl.ds(me, 1), :]
+            col = jnp.transpose(jnp.broadcast_to(row, (own_rows, own_rows)))[:, :1]
+            gate = both[part_rows, pl.ds(0, hidden_units)]
+            up = both[part_rows, pl.ds(hidden_units, hidden_units)]
+            hid[part_rows, :] = (gate / (1.0 + jnp.exp(-gate)) * up * col).astype(hid.dtype)
+
+        def leave(t, carry):
+            cols = pl.ds(pl.multiple_of(t * out_tile, 128), out_tile)
+            made = jnp.dot(hid[...], w_out[:, cols], preferred_element_type=jnp.float32)
+            part[pl.ds(CORES * s, CORES), :, cols] = made.astype(part.dtype).reshape(
+                CORES, own_rows, out_tile
+            )
+            return carry
+
+        lax.fori_loop(0, width // out_tile, leave, 0)
+        near_copy(s).start()
+
+    def near_copy(s):
+        return send(part.at[CORES * s + 1 - q], near.at[s], part_s.at[s], part_r.at[s], sib)
+
+    def pair_sum(s, c):
+        return part[CORES * s + q, rows(c)].astype(jnp.float32) + near[s, rows(c)].astype(jnp.float32)
+
+    def onward(s, c, has_up, came, came_sem, device):
+        @pl.when(c == 0)
+        def _():
+            near_copy(s).wait_recv()
+
+        total[...] = pair_sum(s, c)
+
+        @pl.when(has_up)
+        def _():
+            send(
+                going.at[s, rows(c)], came.at[s, rows(c)], go_s.at[s, c], came_sem.at[s, c], sib
+            ).wait_recv()
+            total[...] += came[s, rows(c)].astype(jnp.float32)
+
+        going[s, rows(c)] = total[...].astype(going.dtype)
+        send(
+            going.at[s, rows(c)], came.at[s, rows(c)], go_s.at[s, c], came_sem.at[s, c], device
+        ).start()
+
+    def slot(k, carry):
+        for side in range(2):
+            s = p - k if side == 0 else p + k
+            valid = (s >= 0) if side == 0 else ((s < chips) & (k > 0))
+
+            @pl.when(valid)
+            def _():
+                sib_wait(s)
+                expert(s)
+
+        def step(i, inner):
+            to_right = i - LAG * p
+
+            @pl.when((p < k) & (to_right >= 0) & (to_right < CHUNKS))
+            def _():
+                onward(k, to_right, has_left, from_left, left_r, right)
+
+            to_left = i - LAG * (chips - 1 - p)
+            low = chips - 1 - k
+
+            @pl.when((p > low) & (to_left >= 0) & (to_left < CHUNKS))
+            def _():
+                onward(low, to_left, has_right, from_right, right_r, left)
+
+            before = p - k - 1
+
+            @pl.when((i < CHUNKS) & (before >= 0))
+            def _():
+                gather_copy(before, i, ag_right, ag_r, sib).wait_recv()
+
+                @pl.when(has_right)
+                def _():
+                    gather_copy(before, i, ag_right, ag_r, right).start()
+
+                gather_copy(before, i, ag_sib, sib_r, sib).start()
+
+            after = p + k + 1
+
+            @pl.when((i < CHUNKS) & (after < chips))
+            def _():
+                gather_copy(after, i, ag_left, ag_r, sib).wait_recv()
+
+                @pl.when(has_left)
+                def _():
+                    gather_copy(after, i, ag_left, ag_r, left).start()
+
+                gather_copy(after, i, ag_sib, sib_r, sib).start()
+
+            return inner
+
+        lax.fori_loop(0, CHUNKS + LAG * (chips - 1), step, 0)
+        return carry
+
+    lax.fori_loop(0, chips, slot, 0)
+    near_copy(p).wait_recv()
+
+    def finish(c, carry):
+        total[...] = pair_sum(p, c)
+
+        @pl.when(has_left)
+        def _():
+            block = from_left.at[p, rows(c)]
+            send(block, block, go_s.at[p, c], left_r.at[p, c], sib).wait_recv()
+            total[...] += from_left[p, rows(c)].astype(jnp.float32)
+
+        @pl.when(has_right)
+        def _():
+            block = from_right.at[p, rows(c)]
+            send(block, block, go_s.at[p, c], right_r.at[p, c], sib).wait_recv()
+            total[...] += from_right[p, rows(c)].astype(jnp.float32)
+
+        out[0, rows(c)] = total[...].astype(out.dtype)
+        return carry
+
+    lax.fori_loop(0, CHUNKS, finish, 0)
+
+    for step in range(1, count):
+        send(scale, scales.at[me], sc_s.at[step], sc_r.at[step], sib).wait_send()
+
+    def drain(s, carry):
+        near_copy(s).wait_send()
+
+        def one(c, inner):
+            gather_copy(s, c, ag_sib, sib_r, sib).wait_send()
+
+            @pl.when(has_right & (s <= p))
+            def _():
+                gather_copy(s, c, ag_right, ag_r, sib).wait_send()
+
+            @pl.when(has_left & (s >= p))
+            def _():
+                gather_copy(s, c, ag_left, ag_r, sib).wait_send()
+
+            @pl.when(s != p)
+            def _():
+                block = going.at[s, rows(c)]
+                send(block, block, go_s.at[s, c], left_r.at[s, c], sib).wait_send()
+
+            return inner
+
+        lax.fori_loop(0, CHUNKS, one, 0)
+        return carry
+
+    lax.fori_loop(0, chips, drain, 0)
+
+
+def scratch_of(chips, own_rows, width, hidden_units, experts_all, dtype):
+    count = chips * CORES
+    blocks = pltpu.VMEM((count, own_rows, width), dtype)
+    halves = pltpu.VMEM((chips, own_rows, width), dtype)
+    dma = pltpu.SemaphoreType.DMA
+    grid = dma((chips, CHUNKS))
+    return [
+        blocks,
+        pltpu.VMEM((width, 2 * hidden_units), dtype),
+        pltpu.VMEM((hidden_units, width), dtype),
+        pltpu.VMEM((count, experts_all, own_rows), jnp.float32),
+        pltpu.VMEM((CORES * own_rows, 2 * hidden_units), jnp.float32),
+        pltpu.VMEM((CORES * own_rows, hidden_units), dtype),
+        blocks,
+        halves,
+        halves,
+        halves,
+        halves,
+        pltpu.VMEM((own_rows // CHUNKS, width), jnp.float32),
+        dma((5,)),
+        dma((count,)),
+        dma((count,)),
+        grid, grid, grid, grid, grid,
+        dma((chips,)),
+        dma((chips,)),
+        grid, grid, grid,
+    ]
+
+
+def line_plan(tokens, w_gate, w_up, w_down, expert_ids, gate_index, gate_table, spill):
+    experts_all = lax.axis_size("expert")
+    own_rows, width = tokens.shape[1:]
+    chips = experts_all // CORES
+    scale = token_scales(
+        expert_ids, gate_index, gate_table, spill, own_rows, experts_all
+    )
+    anywhere = pl.BlockSpec(memory_space=pl.ANY)
+    vmem = pl.BlockSpec(memory_space=pltpu.VMEM)
+    return pl.pallas_call(
+        functools.partial(line_kernel, chips),
+        out_shape=jax.ShapeDtypeStruct(tokens.shape, tokens.dtype),
+        in_specs=[anywhere] * 4 + [vmem],
+        out_specs=vmem,
+        scratch_shapes=scratch_of(
+            chips, own_rows, width, w_gate.shape[2], experts_all, tokens.dtype
+        ),
+        compiler_params=pltpu.CompilerParams(
+            collective_id=0, has_side_effects=True, vmem_limit_bytes=67043328
+        ),
+    )(tokens, w_gate, w_up, w_down, scale)
+
+
+def local(tokens, w_gate, w_up, w_down, *routing):
+    own_rows, width = tokens.shape[1:]
+    experts_all = lax.axis_size("expert")
+    held = w_gate.size + w_up.size + w_down.size + 4 * experts_all * own_rows * width
+    fits = held * tokens.dtype.itemsize <= 56 * 2**20
+    if fits and w_gate.shape[0] == 1 and experts_all % CORES == 0:
+        return line_plan(tokens, w_gate, w_up, w_down, *routing)
+    return exchange_plan(tokens, w_gate, w_up, w_down, *routing)
+
+
 def solution(mesh):
     in_specs = (
         P("expert", "dp", None),

time: 445 us -> 146 us (0.33); the launches traced: 439 us -> 146 us
  blocking collectives: 145 us -> 0 us
  Pallas kernels: 0 us -> 139 us
  waiting for transfers between devices: 127 us -> 0 us
  local copies, waits for them, and re-layouts: 107 us -> 3.63 us
  matrix products: 27.5 us -> 1.52 us
  other arithmetic: 17.9 us -> 1.71 us
  starting transfers between devices: 14.1 us -> 0 us
    all_to_all x1 -> x0, blocking collectives: 145 us -> none  [local(): lax.all_to_all(outbound, 'expert', split_axis=0, concat_axis=0, tiled=True)]
    pallas_call x0 -> x1, Pallas kernels: none -> 139 us  [line_plan(): pl.pallas_call(functools.partial(line_kernel, chips), out_shape=jax.Shape...]
    all_to_all x3 -> x0, waiting for transfers between devices: 127 us -> none  [the longest x1 127 us: local(): lax.all_to_all(expert_out, 'expert', split_axis=0, concat_axis=0, tiled=T...]
    gather x19 -> x0, local copies, waits for them, and re-layouts: 81.8 us -> none  [the longest x8 51.6 us: combine(): results[chosen_slots[:, member]].astype(jnp.float32)]
    dot_general x3 -> x1, matrix products: 27.5 us -> 1.52 us  [token_scales(): jnp.dot(earlier.astype(jnp.bfloat16), chosen.astype(jnp.bfloat16), prefer...]
    all_to_all x3 -> x0, starting transfers between devices: 14.1 us -> none  [the longest x1 5.19 us: local(): lax.all_to_all(outgoing_rows, 'dp', split_axis=0, concat_axis=0, tiled=True)]
    scatter x3 -> x0, local copies, waits for them, and re-layouts: 12.9 us -> none  [the longest x1 8.04 us: local(): dispatch_source = jnp.full((empty_slot,), source_rows.shape[0] - 1, jnp.i...]
    convert_element_type x4 -> x0, other arithmetic: 8.12 us -> none  [the longest x1 4.55 us: local(): return mixed.astype(jnp.bfloat16)[None]]
  transfers between devices with their start and end apart: 3 -> 0, of which waited for: 1 -> 0; matrix products, arithmetic and copies ran while one was open for 15% -> 0% of each run, Pallas kernels for 0% -> 0%
where the time goes in v1:
time: 146 us
  Pallas kernels  139 us (95%)
  local copies, waits for them, and re-layouts  3.63 us (2%)
  other arithmetic  1.71 us (1%)
  matrix products  1.52 us (1%)
    pallas_call x1, Pallas kernels, line_plan(): pl.pallas_call(functools.partial(line_kernel, chips), out_shape=jax.Shape...  139 us

profile of v1, /device:TPU:0, one launch (start us, length us, event | category | flops | bytes accessed | tf_op | source)
XLA Modules:
  0.0 145.8 jit_solution(16818355879070181463)
XLA Ops:
  0.0 0.7 fusion.7
  0.7 0.7 dynamic-slice_bitcast_fusion
  1.3 1.0 select_reduce_fusion
  2.3 0.7 iota_compare_fusion.2
  3.1 1.5 %fusion.scale = f32[8,128]{1,0:T(8,128)} fusion(pred[512,8]{0,1:T(8,128)(4,1)S(1)} %get-tuple-element.8, s32[512]{0:T(512)} %bitcast.10, s32[128]{0:T(128)S(1)} %iota_add_fusion, s32[128]{0:T(128)S(1)} %fusion.7, f32[128,8]{0,1:T(8,128)S(1)} %select_reduce_fusion.2), kind=kOutput, calls=%fused_computation.1 | convolution fusion | flops 1247232 | bytes 15360 | tf_op jit(solution)/shard_map/dot_general | solution.py:146
  4.6 138.9 %shard_map.82 = bf16[1,128,4096]{2,1,0:T(8,128)(2,1)} custom-call(bf16[1,128,4096]{2,1,0:T(8,128)(2,1)} %tok.1, bf16[1,4096,896]{2,1,0:T(8,128)(2,1)} %w_gate.1, bf16[1,4096,896]{2,1,0:T(8,128)(2,1)} %w_up.1, bf16[1,896,4096]{2,1,0:T(8,128)(2,1)} %w_down.1, f32[8,128]{1,0:T(8,128)} %fusion.scale), custom_call_target="tpu_custom_call" | custom-call | tf_op jit(solution)/shard_map/pallas_call | solution.py:439
  143.5 2.3 %copy.13 = bf16[1,128,4096]{2,1,0:T(8,128)(2,1)} copy(bf16[1,128,4096]{2,1,0:T(8,128)(2,1)} %shard_map.82) | data formatting | bytes 2097152
  (3 shorter events, 0.0 us)

commit v2 on v1

--- a/solution.py
+++ b/solution.py
@@ -191,8 +191,8 @@
         pltpu.make_async_copy(w_up.at[0], w_in.at[:, pl.ds(hidden_units, hidden_units)], own_sem.at[3]),
         pltpu.make_async_copy(w_down.at[0], w_out, own_sem.at[4]),
     ]
-    loads[0].start()
-    loads[1].start()
+    for load in loads:
+        load.start()
     barrier = pltpu.get_barrier_semaphore()
     for step in range(1, count):
         pl.semaphore_signal(
@@ -200,28 +200,25 @@
         )
     pl.semaphore_wait(barrier, count - 1)
     loads[0].wait()
-
-    def first_sends(c, carry):
-        @pl.when(has_right)
-        def _():
-            gather_copy(p, c, ag_right, ag_r, right).start()
-
-        @pl.when(has_left)
-        def _():
-            gather_copy(p, c, ag_left, ag_r, left).start()
-
-        gather_copy(p, c, ag_sib, sib_r, sib).start()
-        return carry
-
-    lax.fori_loop(0, CHUNKS, first_sends, 0)
-    loads[1].wait()
     for step in range(1, count):
         send(
             scale, scales.at[me], sc_s.at[step], sc_r.at[step], lax.rem(me + step, count)
         ).start()
-    for load in loads[2:]:
-        load.start()
-    for load in loads[2:]:
+
+    def first_sends(c, carry):
+        @pl.when(has_right)
+        def _():
+            gather_copy(p, c, ag_right, ag_r, right).start()
+
+        @pl.when(has_left)
+        def _():
+            gather_copy(p, c, ag_left, ag_r, left).start()
+
+        gather_copy(p, c, ag_sib, sib_r, sib).start()
+        return carry
+
+    lax.fori_loop(0, CHUNKS, first_sends, 0)
+    for load in loads[1:]:
         load.wait()
     for step in range(1, count):
         send(

time: 146 us -> 134 us (0.918)
  Pallas kernels: 139 us -> 126 us
    pallas_call x1, Pallas kernels: 139 us -> 126 us  [line_plan(): pl.pallas_call(functools.partial(line_kernel, chips), out_shape=jax.Shape...]
where the time goes in v2:
time: 134 us; the launch traced here: 133 us
  Pallas kernels  126 us (94%)
  local copies, waits for them, and re-layouts  3.63 us (3%)
  other arithmetic  1.71 us (1%)
  matrix products  1.52 us (1%)
    pallas_call x1, Pallas kernels, line_plan(): pl.pallas_call(functools.partial(line_kernel, chips), out_shape=jax.Shape...  126 us

profile of v2, /device:TPU:0, one launch (start us, length us, event | category | flops | bytes accessed | tf_op | source)
XLA Modules:
  0.0 133.4 jit_solution(6785479029616487878)
XLA Ops:
  0.0 0.7 fusion.7
  0.7 0.7 dynamic-slice_bitcast_fusion
  1.3 1.0 select_reduce_fusion
  2.3 0.7 iota_compare_fusion.2
  3.1 1.5 %fusion.scale = f32[8,128]{1,0:T(8,128)} fusion(pred[512,8]{0,1:T(8,128)(4,1)S(1)} %get-tuple-element.8, s32[512]{0:T(512)} %bitcast.10, s32[128]{0:T(128)S(1)} %iota_add_fusion, s32[128]{0:T(128)S(1)} %fusion.7, f32[128,8]{0,1:T(8,128)S(1)} %select_reduce_fusion.2), kind=kOutput, calls=%fused_computation.1 | convolution fusion | flops 1247232 | bytes 15360 | tf_op jit(solution)/shard_map/dot_general | solution.py:146
  4.6 126.5 %shard_map.82 = bf16[1,128,4096]{2,1,0:T(8,128)(2,1)} custom-call(bf16[1,128,4096]{2,1,0:T(8,128)(2,1)} %tok.1, bf16[1,4096,896]{2,1,0:T(8,128)(2,1)} %w_gate.1, bf16[1,4096,896]{2,1,0:T(8,128)(2,1)} %w_up.1, bf16[1,896,4096]{2,1,0:T(8,128)(2,1)} %w_down.1, f32[8,128]{1,0:T(8,128)} %fusion.scale), custom_call_target="tpu_custom_call" | custom-call | tf_op jit(solution)/shard_map/pallas_call | solution.py:436
  131.1 2.3 %copy.13 = bf16[1,128,4096]{2,1,0:T(8,128)(2,1)} copy(bf16[1,128,4096]{2,1,0:T(8,128)(2,1)} %shard_map.82) | data formatting | bytes 2097152
  (3 shorter events, 0.0 us)

commit v3 on v2

--- a/solution.py
+++ b/solution.py
@@ -124,7 +124,9 @@
 
 
 CORES = 2
-CHUNKS = 8
+CHUNKS = 4
+TILES = 8
+LEAVE = 4
 LAG = 2
 MESH = pl.DeviceIdType.MESH
 
@@ -163,6 +165,7 @@
     own_rows, width = tok.shape[1], tok.shape[2]
     hidden_units = w_gate.shape[2]
     piece = own_rows // CHUNKS
+    tile = width // TILES
     count = chips * CORES
     me = lax.axis_index("expert")
     p = me // CORES
@@ -226,8 +229,9 @@
         ).wait_recv()
 
     tall = CORES * own_rows
-    in_tile = 2 * hidden_units // 7 if (2 * hidden_units) % 7 == 0 else 2 * hidden_units
-    out_tile = width // 8
+    in_tile = hidden_units
+    out_tile = width // LEAVE
+    per_leave = TILES // LEAVE
 
     def sib_wait(s):
         def one(c, carry):
@@ -253,40 +257,52 @@
             up = both[part_rows, pl.ds(hidden_units, hidden_units)]
             hid[part_rows, :] = (gate / (1.0 + jnp.exp(-gate)) * up * col).astype(hid.dtype)
 
+        def pass_on(first):
+            for c in range(per_leave):
+                @pl.when((p == 0) & (s > p))
+                def _():
+                    onward(s, first + c, None, from_left, left_r, right)
+
+                @pl.when((p == chips - 1) & (s < p))
+                def _():
+                    onward(s, first + c, None, from_right, right_r, left)
+
         def leave(t, carry):
             cols = pl.ds(pl.multiple_of(t * out_tile, 128), out_tile)
             made = jnp.dot(hid[...], w_out[:, cols], preferred_element_type=jnp.float32)
-            part[pl.ds(CORES * s, CORES), :, cols] = made.astype(part.dtype).reshape(
-                CORES, own_rows, out_tile
-            )
+            made = made.astype(part.dtype).reshape(CORES, own_rows, out_tile)
+            for c in range(per_leave):
+                at = t * per_leave + c
+                part[pl.ds(CORES * s, CORES), at] = made[:, :, c * tile : (c + 1) * tile]
+                near_copy(s, at).start()
+
+            @pl.when(t > 0)
+            def _():
+                pass_on((t - 1) * per_leave)
+
             return carry
 
-        lax.fori_loop(0, width // out_tile, leave, 0)
-        near_copy(s).start()
-
-    def near_copy(s):
-        return send(part.at[CORES * s + 1 - q], near.at[s], part_s.at[s], part_r.at[s], sib)
+        lax.fori_loop(0, LEAVE, leave, 0)
+        pass_on(TILES - per_leave)
+
+    def near_copy(s, c):
+        return send(
+            part.at[CORES * s + 1 - q, c], near.at[s, c], part_s.at[s, c], part_r.at[s, c], sib
+        )
 
     def pair_sum(s, c):
-        return part[CORES * s + q, rows(c)].astype(jnp.float32) + near[s, rows(c)].astype(jnp.float32)
-
-    def onward(s, c, has_up, came, came_sem, device):
-        @pl.when(c == 0)
-        def _():
-            near_copy(s).wait_recv()
-
-        total[...] = pair_sum(s, c)
-
-        @pl.when(has_up)
-        def _():
-            send(
-                going.at[s, rows(c)], came.at[s, rows(c)], go_s.at[s, c], came_sem.at[s, c], sib
-            ).wait_recv()
-            total[...] += came[s, rows(c)].astype(jnp.float32)
-
-        going[s, rows(c)] = total[...].astype(going.dtype)
+        near_copy(s, c).wait_recv()
+        return part[CORES * s + q, c].astype(jnp.float32) + near[s, c].astype(jnp.float32)
+
+    def onward(s, c, up_sem, came, came_sem, device):
+        if up_sem is None:
+            going[s, c] = pair_sum(s, c).astype(going.dtype)
+        else:
+            block = going.at[s, c]
+            send(block, came.at[s, c], go_s.at[s, c], up_sem.at[s, c], sib).wait_recv()
+            going[s, c] = (pair_sum(s, c) + came[s, c].astype(jnp.float32)).astype(going.dtype)
         send(
-            going.at[s, rows(c)], came.at[s, rows(c)], go_s.at[s, c], came_sem.at[s, c], device
+            going.at[s, c], came.at[s, c], go_s.at[s, c], came_sem.at[s, c], device
         ).start()
 
     def slot(k, carry):
@@ -300,78 +316,76 @@
                 expert(s)
 
         def step(i, inner):
-            to_right = i - LAG * p
-
-            @pl.when((p < k) & (to_right >= 0) & (to_right < CHUNKS))
-            def _():
-                onward(k, to_right, has_left, from_left, left_r, right)
-
-            to_left = i - LAG * (chips - 1 - p)
+            to_right = i - LAG * (p - 1)
+
+            @pl.when((p > 0) & (p < k) & (to_right >= 0) & (to_right < TILES))
+            def _():
+                onward(k, to_right, left_r, from_left, left_r, right)
+
+            to_left = i - LAG * (chips - 2 - p)
             low = chips - 1 - k
 
-            @pl.when((p > low) & (to_left >= 0) & (to_left < CHUNKS))
-            def _():
-                onward(low, to_left, has_right, from_right, right_r, left)
+            @pl.when((p < chips - 1) & (p > low) & (to_left >= 0) & (to_left < TILES))
+            def _():
+                onward(low, to_left, right_r, from_right, right_r, left)
+
+            turn = TILES // CHUNKS
+            gather = lax.rem(i, turn) == turn - 1
+            g = i // turn
 
             before = p - k - 1
 
-            @pl.when((i < CHUNKS) & (before >= 0))
-            def _():
-                gather_copy(before, i, ag_right, ag_r, sib).wait_recv()
+            @pl.when(gather & (g < CHUNKS) & (before >= 0))
+            def _():
+                gather_copy(before, g, ag_right, ag_r, sib).wait_recv()
 
                 @pl.when(has_right)
                 def _():
-                    gather_copy(before, i, ag_right, ag_r, right).start()
-
-                gather_copy(before, i, ag_sib, sib_r, sib).start()
+                    gather_copy(before, g, ag_right, ag_r, right).start()
+
+                gather_copy(before, g, ag_sib, sib_r, sib).start()
 
             after = p + k + 1
 
-            @pl.when((i < CHUNKS) & (after < chips))
-            def _():
-                gather_copy(after, i, ag_left, ag_r, sib).wait_recv()
+            @pl.when(gather & (g < CHUNKS) & (after < chips))
+            def _():
+                gather_copy(after, g, ag_left, ag_r, sib).wait_recv()
 
                 @pl.when(has_left)
                 def _():
-                    gather_copy(after, i, ag_left, ag_r, left).start()
-
-                gather_copy(after, i, ag_sib, sib_r, sib).start()
+                    gather_copy(after, g, ag_left, ag_r, left).start()
+
+                gather_copy(after, g, ag_sib, sib_r, sib).start()
 
             return inner
 
-        lax.fori_loop(0, CHUNKS + LAG * (chips - 1), step, 0)
+        lax.fori_loop(0, TILES + LAG * max(chips - 2, 0), step, 0)
         return carry
 
     lax.fori_loop(0, chips, slot, 0)
-    near_copy(p).wait_recv()
 
     def finish(c, carry):
         total[...] = pair_sum(p, c)
-
-        @pl.when(has_left)
-        def _():
-            block = from_left.at[p, rows(c)]
-            send(block, block, go_s.at[p, c], left_r.at[p, c], sib).wait_recv()
-            total[...] += from_left[p, rows(c)].astype(jnp.float32)
-
-        @pl.when(has_right)
-        def _():
-            block = from_right.at[p, rows(c)]
-            send(block, block, go_s.at[p, c], right_r.at[p, c], sib).wait_recv()
-            total[...] += from_right[p, rows(c)].astype(jnp.float32)
-
-        out[0, rows(c)] = total[...].astype(out.dtype)
+        for there, came, came_sem in (
+            (has_left, from_left, left_r), (has_right, from_right, right_r)
+        ):
+            @pl.when(there)
+            def _():
+                block = came.at[p, c]
+                send(block, block, go_s.at[p, c], came_sem.at[p, c], sib).wait_recv()
+                total[...] += came[p, c].astype(jnp.float32)
+
+        cols = pl.ds(pl.multiple_of(c * tile, 128), tile)
+        out[0, :, cols] = total[...].astype(out.dtype)
         return carry
 
-    lax.fori_loop(0, CHUNKS, finish, 0)
+    lax.fori_loop(0, TILES, finish, 0)
 
     for step in range(1, count):
         send(scale, scales.at[me], sc_s.at[step], sc_r.at[step], sib).wait_send()
 
     def drain(s, carry):
-        near_copy(s).wait_send()
-
-        def one(c, inner):
+        def gathered(c, inner):
             gather_copy(s, c, ag_sib, sib_r, sib).wait_send()
 
             @pl.when(has_right & (s <= p))
@@ -382,14 +396,20 @@
             def _():
                 gather_copy(s, c, ag_left, ag_r, sib).wait_send()
 
+            return inner
+
+        def summed(c, inner):
+            near_copy(s, c).wait_send()
+
             @pl.when(s != p)
             def _():
-                block = going.at[s, rows(c)]
+                block = going.at[s, c]
                 send(block, block, go_s.at[s, c], left_r.at[s, c], sib).wait_send()
 
             return inner
 
-        lax.fori_loop(0, CHUNKS, one, 0)
+        lax.fori_loop(0, CHUNKS, gathered, 0)
+        lax.fori_loop(0, TILES, summed, 0)
         return carry
 
     lax.fori_loop(0, chips, drain, 0)
@@ -397,30 +417,29 @@
 
 def scratch_of(chips, own_rows, width, hidden_units, experts_all, dtype):
     count = chips * CORES
-    blocks = pltpu.VMEM((count, own_rows, width), dtype)
-    halves = pltpu.VMEM((chips, own_rows, width), dtype)
+    tile = width // TILES
+    halves = pltpu.VMEM((chips, TILES, own_rows, tile), dtype)
     dma = pltpu.SemaphoreType.DMA
-    grid = dma((chips, CHUNKS))
+    gather = dma((chips, CHUNKS))
+    tiled = dma((chips, TILES))
     return [
-        blocks,
+        pltpu.VMEM((count, own_rows, width), dtype),
         pltpu.VMEM((width, 2 * hidden_units), dtype),
         pltpu.VMEM((hidden_units, width), dtype),
         pltpu.VMEM((count, experts_all, own_rows), jnp.float32),
         pltpu.VMEM((CORES * own_rows, 2 * hidden_units), jnp.float32),
         pltpu.VMEM((CORES * own_rows, hidden_units), dtype),
-        blocks,
+        pltpu.VMEM((count, TILES, own_rows, tile), dtype),
         halves,
         halves,
         halves,
         halves,
-        pltpu.VMEM((own_rows // CHUNKS, width), jnp.float32),
+        pltpu.VMEM((own_rows, tile), jnp.float32),
         dma((5,)),
         dma((count,)),
         dma((count,)),
-        grid, grid, grid, grid, grid,
-        dma((chips,)),
-        dma((chips,)),
-        grid, grid, grid,
+        gather, gather, gather, gather, gather,
+        tiled, tiled, tiled, tiled, tiled,
     ]
 
 

time: 134 us -> 129 us (0.963)
  Pallas kernels: 126 us -> 122 us
    pallas_call x1, Pallas kernels: 126 us -> 122 us  [line_plan(): pl.pallas_call(functools.partial(line_kernel, chips), out_shape=jax.Shape...]
where the time goes in v3:
time: 129 us
  Pallas kernels  122 us (95%)
  local copies, waits for them, and re-layouts  3.63 us (3%)
  other arithmetic  1.71 us (1%)
  matrix products  1.52 us (1%)
    pallas_call x1, Pallas kernels, line_plan(): pl.pallas_call(functools.partial(line_kernel, chips), out_shape=jax.Shape...  122 us

profile of v3, /device:TPU:0, one launch (start us, length us, event | category | flops | bytes accessed | tf_op | source)
XLA Modules:
  0.0 128.8 jit_solution(12351855842380375073)
XLA Ops:
  0.0 0.7 fusion.7
  0.7 0.7 dynamic-slice_bitcast_fusion
  1.3 1.0 select_reduce_fusion
  2.3 0.7 iota_compare_fusion.2
  3.1 1.5 %fusion.scale = f32[8,128]{1,0:T(8,128)} fusion(pred[512,8]{0,1:T(8,128)(4,1)S(1)} %get-tuple-element.8, s32[512]{0:T(512)} %bitcast.10, s32[128]{0:T(128)S(1)} %iota_add_fusion, s32[128]{0:T(128)S(1)} %fusion.7, f32[128,8]{0,1:T(8,128)S(1)} %select_reduce_fusion.2), kind=kOutput, calls=%fused_computation.1 | convolution fusion | flops 1247232 | bytes 15360 | tf_op jit(solution)/shard_map/dot_general | solution.py:148
  4.6 121.9 %shard_map.82 = bf16[1,128,4096]{2,1,0:T(8,128)(2,1)} custom-call(bf16[1,128,4096]{2,1,0:T(8,128)(2,1)} %tok.1, bf16[1,4096,896]{2,1,0:T(8,128)(2,1)} %w_gate.1, bf16[1,4096,896]{2,1,0:T(8,128)(2,1)} %w_up.1, bf16[1,896,4096]{2,1,0:T(8,128)(2,1)} %w_down.1, f32[8,128]{1,0:T(8,128)} %fusion.scale), custom_call_target="tpu_custom_call" | custom-call | tf_op jit(solution)/shard_map/pallas_call | solution.py:455
  126.5 2.3 %copy.13 = bf16[1,128,4096]{2,1,0:T(8,128)(2,1)} copy(bf16[1,128,4096]{2,1,0:T(8,128)(2,1)} %shard_map.82) | data formatting | bytes 2097152
  (3 shorter events, 0.0 us)

commit v4 on v3

--- a/solution.py
+++ b/solution.py
@@ -132,33 +132,46 @@
 
 
 def token_scales(expert_ids, gate_index, gate_table, spill, own_rows, experts_all):
-    top_count = expert_ids.shape[2]
-    column_tokens = spill.shape[1]
+    top_count, column_tokens = expert_ids.shape[1:]
     capacity = 3 * own_rows * top_count // (2 * experts_all)
-    first = lax.axis_index("dp") * own_rows
-    senders = spill[0]
-    experts = jnp.arange(experts_all, dtype=jnp.int32)
-    hot = expert_ids[0][:, :, None] == experts
-    chosen = jnp.any(hot, axis=1)
-    own_senders = lax.dynamic_slice_in_dim(senders, first, own_rows)
-    own_tokens = first + jnp.arange(own_rows, dtype=jnp.int32)
-    earlier = (jnp.arange(column_tokens, dtype=jnp.int32)[None, :] < own_tokens[:, None]) & (
-        senders[None, :] == own_senders[:, None]
-    )
-    rank = jnp.dot(
-        earlier.astype(jnp.bfloat16), chosen.astype(jnp.bfloat16), preferred_element_type=jnp.float32
-    )
-    own_index = lax.dynamic_slice_in_dim(gate_index[0], first, own_rows)
-    levels = jnp.arange(gate_table.shape[0], dtype=jnp.int32)
-    picked = jnp.sum(jnp.where(own_index[:, :, None] == levels, gate_table, 0.0), axis=2)
-    weight = picked / jnp.sum(picked, axis=1, keepdims=True)
-    own_hot = lax.dynamic_slice_in_dim(hot, first, own_rows)
-    scale = jnp.sum(jnp.where(own_hot, weight[:, :, None], 0.0), axis=1)
-    return jnp.where(rank < capacity, scale, 0.0).T
+    first = pl.multiple_of(lax.axis_index("dp") * own_rows, own_rows)
+    own = pl.ds(first, own_rows)
+    experts = lax.broadcasted_iota(jnp.int32, (experts_all, column_tokens), 0)
+    chosen = jnp.zeros((experts_all, column_tokens), jnp.float32)
+    for k in range(top_count):
+        chosen += jnp.where(expert_ids[0, k : k + 1, :] == experts, 1.0, 0.0)
+    own_row = spill[:, own].astype(jnp.float32)
+    own_senders = jnp.transpose(jnp.broadcast_to(own_row, (own_rows, own_rows)))[:, :1]
+    shape = (own_rows, column_tokens)
+    before = lax.broadcasted_iota(jnp.int32, shape, 1) < first + lax.broadcasted_iota(
+        jnp.int32, shape, 0
+    )
+    earlier = before & (spill[...].astype(jnp.float32) == own_senders)
+    rank = lax.dot_general(
+        chosen.astype(jnp.bfloat16),
+        jnp.where(earlier, 1.0, 0.0).astype(jnp.bfloat16),
+        (((1,), (1,)), ((), ())),
+        preferred_element_type=jnp.float32,
+    )
+    level_count = gate_table.shape[1]
+    levels = lax.broadcasted_iota(jnp.int32, (level_count, own_rows), 0)
+    table = jnp.transpose(jnp.broadcast_to(gate_table[...], (own_rows, level_count)))
+    picked = [
+        jnp.sum(
+            jnp.where(gate_index[0, k : k + 1, own] == levels, table, 0.0), axis=0, keepdims=True
+        )
+        for k in range(top_count)
+    ]
+    norm = functools.reduce(jnp.add, picked)
+    own_experts = lax.broadcasted_iota(jnp.int32, (experts_all, own_rows), 0)
+    scale = jnp.zeros((experts_all, own_rows), jnp.float32)
+    for k in range(top_count):
+        scale += jnp.where(expert_ids[0, k : k + 1, own] == own_experts, picked[k] / norm, 0.0)
+    return jnp.where(rank < capacity, scale, 0.0)
 
 
 def line_kernel(
-    chips, tok, w_gate, w_up, w_down, scale, out,
+    chips, tok, w_gate, w_up, w_down, expert_ids, gate_index, gate_table, spill, out,
     x, w_in, w_out, scales, both, hid, part, near, from_left, from_right, going, total,
     own_sem, sc_s, sc_r, ag_right, ag_left, ag_r, ag_sib, sib_r, part_s, part_r, go_s, left_r, right_r,
 ):
@@ -189,10 +202,9 @@
 
     loads = [
         pltpu.make_async_copy(tok.at[0], x.at[me], own_sem.at[0]),
-        pltpu.make_async_copy(scale, scales.at[me], own_sem.at[1]),
-        pltpu.make_async_copy(w_gate.at[0], w_in.at[:, pl.ds(0, hidden_units)], own_sem.at[2]),
-        pltpu.make_async_copy(w_up.at[0], w_in.at[:, pl.ds(hidden_units, hidden_units)], own_sem.at[3]),
-        pltpu.make_async_copy(w_down.at[0], w_out, own_sem.at[4]),
+        pltpu.make_async_copy(w_gate.at[0], w_in.at[:, pl.ds(0, hidden_units)], own_sem.at[1]),
+        pltpu.make_async_copy(w_up.at[0], w_in.at[:, pl.ds(hidden_units, hidden_units)], own_sem.at[2]),
+        pltpu.make_async_copy(w_down.at[0], w_out, own_sem.at[3]),
     ]
     for load in loads:
         load.start()
@@ -203,10 +215,6 @@
         )
     pl.semaphore_wait(barrier, count - 1)
     loads[0].wait()
-    for step in range(1, count):
-        send(
-            scale, scales.at[me], sc_s.at[step], sc_r.at[step], lax.rem(me + step, count)
-        ).start()
 
     def first_sends(c, carry):
         @pl.when(has_right)
@@ -220,12 +228,17 @@
         gather_copy(p, c, ag_sib, sib_r, sib).start()
         return carry
 
-    lax.fori_loop(0, CHUNKS, first_sends, 0)
+    lax.fori_loop(0, 1, first_sends, 0)
+    scales[me] = token_scales(expert_ids, gate_index, gate_table, spill, tok.shape[1], count)
+    mine = scales.at[me]
+    for step in range(1, count):
+        send(mine, mine, sc_s.at[step], sc_r.at[step], lax.rem(me + step, count)).start()
+    lax.fori_loop(1, CHUNKS, first_sends, 0)
     for load in loads[1:]:
         load.wait()
     for step in range(1, count):
         send(
-            scale, scales.at[lax.rem(me - step + count, count)], sc_s.at[step], sc_r.at[step], sib
+            mine, scales.at[lax.rem(me - step + count, count)], sc_s.at[step], sc_r.at[step], sib
         ).wait_recv()
 
     tall = CORES * own_rows
@@ -382,7 +395,7 @@
     lax.fori_loop(0, TILES, finish, 0)
 
     for step in range(1, count):
-        send(scale, scales.at[me], sc_s.at[step], sc_r.at[step], sib).wait_send()
+        send(mine, mine, sc_s.at[step], sc_r.at[step], sib).wait_send()
 
     def drain(s, carry):
         def gathered(c, inner):
@@ -435,7 +448,7 @@
         halves,
         halves,
         pltpu.VMEM((own_rows, tile), jnp.float32),
-        dma((5,)),
+        dma((4,)),
         dma((count,)),
         dma((count,)),
         gather, gather, gather, gather, gather,
@@ -447,15 +460,12 @@
     experts_all = lax.axis_size("expert")
     own_rows, width = tokens.shape[1:]
     chips = experts_all // CORES
-    scale = token_scales(
-        expert_ids, gate_index, gate_table, spill, own_rows, experts_all
-    )
     anywhere = pl.BlockSpec(memory_space=pl.ANY)
     vmem = pl.BlockSpec(memory_space=pltpu.VMEM)
     return pl.pallas_call(
         functools.partial(line_kernel, chips),
         out_shape=jax.ShapeDtypeStruct(tokens.shape, tokens.dtype),
-        in_specs=[anywhere] * 4 + [vmem],
+        in_specs=[anywhere] * 4 + [vmem] * 4,
         out_specs=vmem,
         scratch_shapes=scratch_of(
             chips, own_rows, width, w_gate.shape[2], experts_all, tokens.dtype
@@ -463,7 +473,10 @@
         compiler_params=pltpu.CompilerParams(
             collective_id=0, has_side_effects=True, vmem_limit_bytes=67043328
         ),
-    )(tokens, w_gate, w_up, w_down, scale)
+    )(
+        tokens, w_gate, w_up, w_down,
+        jnp.swapaxes(expert_ids, 1, 2), jnp.swapaxes(gate_index, 1, 2), gate_table[None], spill,
+    )
 
 
 def local(tokens, w_gate, w_up, w_down, *routing):

time: 129 us -> 125 us (0.969)
  other arithmetic: 1.71 us -> 0 us
  matrix products: 1.52 us -> 0 us
  local copies, waits for them, and re-layouts: 3.63 us -> 2.29 us
    dot_general x1 -> x0, matrix products: 1.52 us -> none  [token_scales(): jnp.dot(earlier.astype(jnp.bfloat16), chosen.astype(jnp.bfloat16), prefer...]
    eq x2 -> x0, local copies, waits for them, and re-layouts: 1.34 us -> none  [the longest x1 0.68 us: token_scales(): own_index[:, :, None] == levels]
where the time goes in v4:
time: 125 us
  Pallas kernels  122 us (98%)
  local copies, waits for them, and re-layouts  2.29 us (2%)
    pallas_call x1, Pallas kernels, line_plan(): pl.pallas_call(functools.partial(line_kernel, chips), out_shape=jax.Shape...  122 us

profile of v4, /device:TPU:0, one launch (start us, length us, event | category | flops | bytes accessed | tf_op | source)
XLA Modules:
  0.0 124.6 jit_solution(13771073594467266375)
XLA Ops:
  0.0 122.3 %shard_map.82 = bf16[1,128,4096]{2,1,0:T(8,128)(2,1)} custom-call(bf16[1,128,4096]{2,1,0:T(8,128)(2,1)} %tok.1, bf16[1,4096,896]{2,1,0:T(8,128)(2,1)} %w_gate.1, bf16[1,4096,896]{2,1,0:T(8,128)(2,1)} %w_up.1, bf16[1,896,4096]{2,1,0:T(8,128)(2,1)} %w_down.1, s32[1,4,512]{2,1,0:T(4,128)} %bitcast.3, s32[1,4,512]{2,1,0:T(4,128)} %bitcast.4, f32[1,256]{1,0:T(1,128)} %bitcast.5, ...), custom_call_target="tpu_custom_call" | custom-call | tf_op jit(solution)/shard_map/pallas_call | solution.py:465
  122.3 2.3 %copy.10 = bf16[1,128,4096]{2,1,0:T(8,128)(2,1)} copy(bf16[1,128,4096]{2,1,0:T(8,128)(2,1)} %shard_map.82) | data formatting | bytes 2097152
